TPU v7x, 32 devices: a whole 2x2x4 slice. The times are simulated.
32 devices in a mesh: band: 4 (over x, core), fft: 8 (over z, y).
Axes of the slice: x: 2, y: 2, z: 4, core: 2. Of those that a mesh axis runs over, the one named last changes fastest.
Arguments:
- orbitals: bfloat16 [16, 2, 32768], P('band', None, 'fft'), may hold values from -6 to 6
- sphere_slot: int32 [32768], P('fft'), may hold values from 0 to 24575, as said below
- stick_column: int32 [1024], P('fft'), may hold values from 0 to 36863, as said below
- potential: float32 [192, 192, 192], P('fft'), may hold values from -3 to 3
- subspace: bfloat16 [64, 2, 32768], P('band', None, 'fft'), may hold values from -0.03125 to 0.03125
- previous: bfloat16 [16, 2, 32768], P('band', None, 'fft'), may hold values from -6 to 6
Outputs:
- applied: bfloat16 [16, 2, 32768], P('band', None, 'fft')
- intersection: float32 [2, 64, 16], P(None, 'fft', 'band')
Inputs may be any that keep to these rules, and one draw needn't show every extreme that they name: `sphere_slot`: within each aligned block of 4096 entries the values are distinct. `stick_column`: aligned block d of 128 entries holds distinct columns x * 192 + y with d * 24 <= x < (d + 1) * 24.
All inputs are finite; a program needn't handle non-finite values.
Results may differ from a plain program's by a relative error of at most 0.012.
Values may be sent and summed in bfloat16 or wider, within the bound.
A program may use at most 64 MiB of HBM per device.

v0:
```python
import functools
import math

import jax
import jax.numpy as jnp
import numpy as np
from jax import lax
from jax.experimental import pallas as pl
from jax.experimental.pallas import tpu as pltpu
from jax.sharding import PartitionSpec as P


def dft_table(length, sign_value, factor):
    positions = jnp.arange(length, dtype=jnp.int32)
    phase_step = positions[:, None] * positions[None, :] % length
    angle_value = phase_step.astype(jnp.float32) * (2.0 * math.pi / length)
    cosine = (jnp.cos(angle_value) * factor).astype(jnp.bfloat16)
    sine_part = (jnp.sin(angle_value) * (sign_value * factor)).astype(jnp.bfloat16)
    return (cosine, sine_part)


def apply_dft(real_in, imag_in, table, form):
    cosine, sine_part = table

    def product(operand, table_part):
        return jnp.einsum(form, operand, table_part, preferred_element_type=jnp.float32)

    real_out = product(real_in, cosine) - product(imag_in, sine_part)
    imag_out = product(real_in, sine_part) + product(imag_in, cosine)
    return (real_out, imag_out)


def packed(pair, axis_pos):
    return jnp.stack([pair[0].astype(jnp.bfloat16), pair[1].astype(jnp.bfloat16)], axis=axis_pos)


def frequency(values, grid_size):
    return jnp.where(values >= grid_size // 2, values - grid_size, values).astype(jnp.float32)


def one_hot_rows(indices, count):
    return (indices[None, :] == jnp.arange(count, dtype=jnp.int32)[:, None]).astype(jnp.bfloat16)


def general_device(orbitals, sphere_slot, stick_column, potential, subspace, previous):
    slab_depth = potential.shape[0]
    grid_size = potential.shape[1]
    stick_count = stick_column.shape[0]
    slab_cells = slab_depth * grid_size
    forward = dft_table(grid_size, 1.0, 1.0)
    inverse = dft_table(grid_size, -1.0, 1.0 / grid_size)
    plane_index = sphere_slot // stick_count
    stick_index = sphere_slot % stick_count
    plane_hot = one_hot_rows(plane_index, grid_size)
    stick_hot = one_hot_rows(stick_index, stick_count)
    stick_coords = jnp.stack([stick_column // grid_size, stick_column % grid_size]).astype(
        jnp.bfloat16
    )
    wave_coords = jnp.dot(stick_coords, stick_hot, preferred_element_type=jnp.float32)
    freq_z = frequency(plane_index, grid_size)
    freq_x = frequency(wave_coords[0].astype(jnp.int32), grid_size)
    freq_y = frequency(wave_coords[1].astype(jnp.int32), grid_size)
    kinetic = (freq_z * freq_z + freq_x * freq_x + freq_y * freq_y) * (
        2.0 / (grid_size * grid_size)
    )
    prev_real = previous[:, 0]
    prev_imag = previous[:, 1]
    sub_piece = lax.all_gather(subspace, "band", axis=0, tiled=True)
    sub_real = sub_piece[:, 0]
    sub_imag = sub_piece[:, 1]
    over_real = jnp.einsum(
        "jg,ig->ji", sub_real, prev_real, preferred_element_type=jnp.float32
    ) + jnp.einsum("jg,ig->ji", sub_imag, prev_imag, preferred_element_type=jnp.float32)
    over_imag = jnp.einsum(
        "jg,ig->ji", sub_real, prev_imag, preferred_element_type=jnp.float32
    ) - jnp.einsum("jg,ig->ji", sub_imag, prev_real, preferred_element_type=jnp.float32)
    partial_value = jnp.stack([over_real, over_imag])
    intersection = lax.psum_scatter(partial_value, "fft", scatter_dimension=1, tiled=True)
    stick_buffer = jnp.einsum(
        "bpi,zi,si->bpzs", orbitals, plane_hot, stick_hot, preferred_element_type=jnp.float32
    ).astype(jnp.bfloat16)

    def potential_work(along_y):
        along_x = apply_dft(along_y[0], along_y[1], forward, "zxy,xk->zky")
        weighted = packed((along_x[0] * potential, along_x[1] * potential), 0)
        back_x = packed(apply_dft(weighted[0], weighted[1], inverse, "zxy,xk->zky"), 0)
        return packed(apply_dft(back_x[0], back_x[1], inverse, "zxy,yk->zxk"), 0)

    along_z = packed(apply_dft(stick_buffer[:, 0], stick_buffer[:, 1], forward, "bzs,zk->bks"), 1)
    all_columns = lax.all_gather(stick_column, "fft", axis=0, tiled=True)
    owners = all_columns.shape[0] // stick_count
    block_columns = (all_columns % slab_cells).reshape(owners, stick_count)
    block_hot = (
        block_columns[:, :, None] == jnp.arange(slab_cells, dtype=jnp.int32)[None, None, :]
    ).astype(jnp.bfloat16)

    def stick_work(one_band):
        plane_depth = one_band.shape[1]
        split_band = one_band.reshape(2, plane_depth, owners, stick_count)
        plane_grid = jnp.einsum(
            "pzds,dsc->pzdc", split_band, block_hot, preferred_element_type=jnp.float32
        ).astype(jnp.bfloat16)
        plane_grid = plane_grid.reshape(2, plane_depth, grid_size, grid_size)
        along_y = packed(apply_dft(plane_grid[0], plane_grid[1], forward, "zxy,yk->zxk"), 0)
        back_y = potential_work(along_y)
        back_split = back_y.reshape(2, plane_depth, owners, slab_cells)
        picked = jnp.einsum(
            "pzdc,dsc->pzds", back_split, block_hot, preferred_element_type=jnp.float32
        ).astype(jnp.bfloat16)
        return picked.reshape(2, plane_depth, owners * stick_count)

    finished = lax.map(
        stick_work, lax.all_to_all(along_z, "fft", split_axis=2, concat_axis=3, tiled=True)
    )
    stick_values = lax.all_to_all(finished, "fft", split_axis=3, concat_axis=2, tiled=True)
    picked_sticks = jnp.einsum(
        "bpzs,si->bpzi", stick_values, stick_hot, preferred_element_type=jnp.float32
    ).astype(jnp.bfloat16)
    cosine_cols = jnp.einsum("zk,ki->zi", inverse[0], plane_hot, preferred_element_type=jnp.float32)
    sine_cols = jnp.einsum("zk,ki->zi", inverse[1], plane_hot, preferred_element_type=jnp.float32)
    pick_real = picked_sticks[:, 0].astype(jnp.float32)
    pick_imag = picked_sticks[:, 1].astype(jnp.float32)
    wave_real = jnp.sum(pick_real * cosine_cols[None] - pick_imag * sine_cols[None], axis=1)
    wave_imag = jnp.sum(pick_real * sine_cols[None] + pick_imag * cosine_cols[None], axis=1)
    real_out = wave_real + kinetic * orbitals[:, 0].astype(jnp.float32)
    imag_out = wave_imag + kinetic * orbitals[:, 1].astype(jnp.float32)
    applied = jnp.stack([real_out, imag_out], axis=1).astype(jnp.bfloat16)
    return (applied, intersection)


PLANES = 4
EXTRA = 16


def phases(products, length):
    angle = (products % length).astype(np.float64) * (2.0 * np.pi / length)
    return np.cos(angle), np.sin(angle)


def line_tables(length):
    cosine, sine = phases(np.outer(np.arange(length), np.arange(length)), length)
    wide = -(-length // 128) * 128
    empty = np.zeros((length, wide - length))
    from_real = np.concatenate([cosine, empty, sine, empty], axis=1)
    from_imag = np.concatenate([-sine, empty, cosine, empty], axis=1)
    return jnp.asarray(np.stack([from_real, from_imag]), jnp.bfloat16)


def half_tables(length):
    half = np.arange(length // 2)
    tables = []
    for parity in (0, 1):
        cosine, sine = phases(np.outer(2 * half + parity, half), length)
        tables.append(np.block([[cosine, -sine], [sine, cosine]]))
    tables.extend([tables[0].T, tables[1].T])
    return jnp.asarray(np.stack(tables), jnp.bfloat16)


def plane_kernel(
    slab, stick_ref, pot_ref, line_ref, half_ref, out_ref, rows_ref, real_ref, imag_ref
):
    group = pl.program_id(0)
    owners, _, sticks = stick_ref.shape
    lines, size, _ = real_ref.shape
    half = size // 2
    wide = line_ref.shape[2] // 2
    part_rows = out_ref.shape[1] // 2
    first = pl.multiple_of(group * lines, lines)
    second = pl.multiple_of(part_rows + group * lines, lines)
    scale = 1.0 / (size * size)

    def stick_mask(owner):
        coords = stick_ref[owner, 2 * part_rows : 2 * part_rows + EXTRA, :].astype(jnp.float32)
        local = lax.broadcasted_iota(jnp.int32, (slab, sticks), 0).astype(jnp.float32)
        return coords[0:1, :] == local

    @pl.when(group == 0)
    def _():
        @pl.loop(0, owners)
        def _(owner):
            coords = stick_ref[owner, 2 * part_rows : 2 * part_rows + EXTRA, :].astype(jnp.float32)
            cells = lax.broadcasted_iota(jnp.int32, (size, sticks), 0).astype(jnp.float32)
            hot = jnp.where(coords[1:2, :] == cells, 1.0, 0.0).astype(jnp.bfloat16)
            for part in range(2):
                rows = lax.dot_general(
                    hot, line_ref[part], (((0,), (0,)), ((), ())),
                    preferred_element_type=jnp.float32,
                )
                rows_ref[owner, part * sticks : (part + 1) * sticks, :] = rows.astype(jnp.bfloat16)

    @pl.loop(0, owners)
    def _(owner):
        mask = stick_mask(owner)[None]
        spread = []
        for start in (first, second):
            values = stick_ref[owner, pl.ds(start, lines), :].astype(jnp.float32)
            spread.append(jnp.where(mask, values[:, None, :], 0.0).reshape(lines * slab, sticks))
        left = jnp.concatenate(spread, axis=1).astype(jnp.bfloat16)
        result = jnp.dot(left, rows_ref[owner], preferred_element_type=jnp.float32)
        place = pl.ds(pl.multiple_of(owner * slab, 8), slab)
        real_ref[:, place, :] = result[:, :size].reshape(lines, slab, size)
        imag_ref[:, place, :] = result[:, wide : wide + size].reshape(lines, slab, size)

    def one_plane(line, plane):
        real_low, real_high = real_ref[line, :half, :], real_ref[line, half:, :]
        imag_low, imag_high = imag_ref[line, :half, :], imag_ref[line, half:, :]
        total = jnp.concatenate([real_low + real_high, imag_low + imag_high], axis=0)
        differ = jnp.concatenate([real_low - real_high, imag_low - imag_high], axis=0)

        def there_and_back(values, parity):
            forward = jnp.dot(
                half_ref[parity], values.astype(jnp.bfloat16), preferred_element_type=jnp.float32
            )
            local = pot_ref[plane, parity]
            weighted = jnp.concatenate([forward[:half] * local, forward[half:] * local], axis=0)
            return jnp.dot(
                half_ref[2 + parity],
                weighted.astype(jnp.bfloat16),
                preferred_element_type=jnp.float32,
            )

        even = there_and_back(total, 0)
        odd = there_and_back(differ, 1)
        low, high = even + odd, even - odd
        real_ref[line, :half, :] = low[:half]
        imag_ref[line, :half, :] = low[half:]
        real_ref[line, half:, :] = high[:half]
        imag_ref[line, half:, :] = high[half:]

    bands = lines // PLANES

    @pl.loop(0, PLANES)
    def _(plane):
        for band in range(bands):
            one_plane(plane * bands + band, plane)

    @pl.loop(0, owners)
    def _(owner):
        mask = stick_mask(owner)[None]
        place = pl.ds(pl.multiple_of(owner * slab, 8), slab)
        real = real_ref[:, place, :].reshape(lines * slab, size).astype(jnp.bfloat16)
        imag = imag_ref[:, place, :].reshape(lines * slab, size).astype(jnp.bfloat16)
        across = (((1,), (1,)), ((), ()))
        result = lax.dot_general(
            real, rows_ref[owner, :, :size], across, preferred_element_type=jnp.float32
        ) + lax.dot_general(
            imag, rows_ref[owner, :, wide : wide + size], across, preferred_element_type=jnp.float32
        )
        result = result.reshape(lines, slab, 2 * sticks)
        for part, start in enumerate((first, second)):
            chosen = result[:, :, part * sticks : (part + 1) * sticks]
            picked = jnp.sum(jnp.where(mask, chosen, 0.0), axis=1) * scale
            out_ref[owner, pl.ds(start, lines), :] = picked.astype(jnp.bfloat16)


def plane_work(received, potential, bands):
    owners, _, sticks = received.shape
    slab, size, _ = potential.shape
    lines = PLANES * bands
    split_pot = potential.reshape(slab, size // 2, 2, size).transpose(0, 2, 1, 3)
    lines_table = line_tables(size)
    halves = half_tables(size)
    wide = lines_table.shape[2]

    def whole(array):
        return pl.BlockSpec(array.shape, lambda g: (0,) * array.ndim)

    rows = 2 * slab * bands
    return pl.pallas_call(
        lambda *refs: plane_kernel(slab, *refs),
        grid=(slab // PLANES,),
        out_shape=jax.ShapeDtypeStruct((owners, rows, sticks), jnp.bfloat16),
        in_specs=[
            whole(received),
            pl.BlockSpec((PLANES, 2, size // 2, size), lambda g: (g, 0, 0, 0)),
            whole(lines_table),
            whole(halves),
        ],
        out_specs=pl.BlockSpec((owners, rows, sticks), lambda g: (0, 0, 0)),
        scratch_shapes=[
            pltpu.VMEM((owners, 2 * sticks, wide), jnp.bfloat16),
            pltpu.VMEM((lines, size, size), jnp.float32),
            pltpu.VMEM((lines, size, size), jnp.float32),
        ],
        compiler_params=pltpu.CompilerParams(
            dimension_semantics=("arbitrary",), vmem_limit_bytes=48 * 1024 * 1024
        ),
        cost_estimate=pl.CostEstimate(
            flops=40 * 10**9, bytes_accessed=8 * 10**6, transcendentals=0
        ),
    )(received, split_pot, lines_table, halves)


def gathered_bands(array, mesh_bands):
    here = lax.axis_index("band")
    blocks = [array]
    for shift in range(1, mesh_bands):
        pairs = [((src + shift) % mesh_bands, src) for src in range(mesh_bands)]
        blocks.append(lax.ppermute(array, "band", pairs))
    return blocks, here


def overlaps(subspace, previous, mesh_bands, owners):
    blocks, here = gathered_bands(subspace, mesh_bands)
    prev_real, prev_imag = previous[:, 0], previous[:, 1]
    right = jnp.concatenate(
        [
            jnp.concatenate([prev_real, prev_imag], axis=1),
            jnp.concatenate([prev_imag, -prev_real], axis=1),
        ],
        axis=0,
    )
    partials = []
    for block in blocks:
        partials.append(
            jnp.einsum(
                "jg,ig->ji",
                block.reshape(block.shape[0], -1),
                right,
                preferred_element_type=jnp.float32,
            )
        )
    twice = jnp.concatenate(partials + partials, axis=0)
    count = twice.shape[0] // 2
    start = (count - here * subspace.shape[0]) % count
    ordered = lax.dynamic_slice_in_dim(twice, start, count, axis=0)
    split = ordered.reshape(owners, count // owners, 2, previous.shape[0])
    return split.transpose(0, 2, 1, 3)


def fast_device(mesh_bands, orbitals, sphere_slot, stick_column, potential, subspace, previous):
    slab_depth, grid_size, _ = potential.shape
    stick_count = stick_column.shape[0]
    owners = grid_size // slab_depth
    bands = orbitals.shape[0]
    forward = dft_table(grid_size, 1.0, 1.0)
    inverse = dft_table(grid_size, -1.0, 1.0 / grid_size)
    plane_index = sphere_slot // stick_count
    stick_index = sphere_slot % stick_count
    plane_hot = one_hot_rows(plane_index, grid_size)
    stick_hot = one_hot_rows(stick_index, stick_count)
    stick_x = stick_column // grid_size
    stick_y = stick_column % grid_size
    stick_coords = jnp.stack([stick_x, stick_y]).astype(jnp.bfloat16)
    wave_coords = jnp.dot(stick_coords, stick_hot, preferred_element_type=jnp.float32)
    freq_z = frequency(plane_index, grid_size)
    freq_x = frequency(wave_coords[0].astype(jnp.int32), grid_size)
    freq_y = frequency(wave_coords[1].astype(jnp.int32), grid_size)
    kinetic = (freq_z * freq_z + freq_x * freq_x + freq_y * freq_y) * (
        2.0 / (grid_size * grid_size)
    )
    local_x = stick_x - lax.axis_index("fft") * slab_depth
    coords = jnp.stack([local_x, stick_y]).astype(jnp.bfloat16)
    coords = jnp.pad(coords, ((0, EXTRA - 2), (0, 0)))
    coords = jnp.broadcast_to(coords[None], (owners, EXTRA, stick_count))
    stick_buffer = jnp.einsum(
        "bpi,zi,si->pzbs", orbitals, plane_hot, stick_hot, preferred_element_type=jnp.float32
    ).astype(jnp.bfloat16)
    along_z = apply_dft(stick_buffer[0], stick_buffer[1], forward, "zbs,zk->kbs")
    pieces = [part.astype(jnp.bfloat16).reshape(owners, -1, stick_count) for part in along_z]
    sent = jnp.concatenate(pieces + [coords], axis=1)
    received = lax.all_to_all(sent, "fft", split_axis=0, concat_axis=0, tiled=True)
    planes = plane_work(received, potential, bands)
    split = overlaps(subspace, previous, mesh_bands, owners)
    flat = split.reshape(owners, 1, -1)
    high = lax.reduce_precision(flat, 8, 7)
    low = lax.reduce_precision(flat - high, 8, 7)
    both = jnp.concatenate([high, low], axis=2).astype(jnp.bfloat16)
    width = both.shape[2]
    lanes = -(-width // stick_count) * stick_count
    both = jnp.pad(both, ((0, 0), (0, 0), (0, lanes - width)))
    both = both.reshape(owners, -1, stick_count)
    both = jnp.pad(both, ((0, 0), (0, EXTRA - both.shape[1]), (0, 0)))
    returned = lax.all_to_all(
        jnp.concatenate([planes, both], axis=1), "fft", split_axis=0, concat_axis=0, tiled=True
    )
    rows = planes.shape[1]
    sums = returned[:, rows:].reshape(owners, -1)[:, :width].astype(jnp.float32)
    sums = jnp.sum(sums, axis=0)
    intersection = (sums[: width // 2] + sums[width // 2 :]).reshape(split.shape[1:])
    stick_values = returned[:, :rows].reshape(owners, 2, slab_depth, bands, stick_count)
    picked = jnp.einsum(
        "dpzbs,si->pdzbi", stick_values, stick_hot, preferred_element_type=jnp.float32
    ).astype(jnp.bfloat16)
    picked = picked.reshape(2, grid_size, bands, -1)
    cosine_cols = jnp.einsum("zk,ki->zi", inverse[0], plane_hot, preferred_element_type=jnp.float32)
    sine_cols = jnp.einsum("zk,ki->zi", inverse[1], plane_hot, preferred_element_type=jnp.float32)
    pick_real = picked[0].astype(jnp.float32)
    pick_imag = picked[1].astype(jnp.float32)
    cosine_cols = cosine_cols[:, None]
    sine_cols = sine_cols[:, None]
    wave_real = jnp.sum(pick_real * cosine_cols - pick_imag * sine_cols, axis=0)
    wave_imag = jnp.sum(pick_real * sine_cols + pick_imag * cosine_cols, axis=0)
    real_out = wave_real + kinetic * orbitals[:, 0].astype(jnp.float32)
    imag_out = wave_imag + kinetic * orbitals[:, 1].astype(jnp.float32)
    applied = jnp.stack([real_out, imag_out], axis=1).astype(jnp.bfloat16)
    return (applied, intersection)


def per_device(mesh_bands, *arrays):
    orbitals, _, _, potential, _, previous = arrays
    slab_depth = potential.shape[0]
    bands = orbitals.shape[0]
    aligned = slab_depth % 8 == 0 and slab_depth % PLANES == 0
    if aligned and PLANES * bands % 16 == 0 and arrays[2].shape[0] % 128 == 0:
        return fast_device(mesh_bands, *arrays)
    return general_device(*arrays)


def solution(mesh):
    return jax.shard_map(
        functools.partial(per_device, mesh.shape["band"]),
        mesh=mesh,
        in_specs=(
            P("band", None, "fft"),
            P("fft"),
            P("fft"),
            P("fft", None, None),
            P("band", None, "fft"),
            P("band", None, "fft"),
        ),
        out_specs=(P("band", None, "fft"), P(None, "fft", "band")),
        check_vma=False,
    )
```

profile of v0, /device:TPU:0, one launch (start us, length us, event | category | flops | bytes accessed | tf_op | source)
XLA Modules:
  0.0 117.3 jit_solution(4958185769448779634)
XLA Ops:
  0.6 2.5 %collective-permute-start = (bf16[16,2,4096]{2,1,0:T(2,128)(2,1)}, bf16[16,2,4096]{2,1,0:T(2,128)(2,1)S(1)}, u32[]{:S(2)}, u32[]{:S(2)}) collective-permute-start(bf16[16,2,4096]{2,1,0:T(2,128)(2,1)} %param.12), channel_id=1, source_target_pairs={{8,0},{16,8},{24,16},{0,24},{9,1},{17,9},{25,17},{1,25},{10,2},{18... | collective-permute-start | bytes 786440 | tf_op jit(solution)/shard_map/ppermute | solution.py:299
  3.1 0.0 collective-permute-start.2
  3.1 1.1 collective-permute-start.1
  4.2 0.7 add_select_fusion.2
  4.9 0.9 convert_bitcast_fusion.2
  5.8 0.2 convert_bitcast_fusion.1
  6.0 0.0 copy-start.8
  6.0 2.9 %fusion.24 = bf16[2,192,4,128]{3,1,0,2:T(8,128)(2,1)S(1)} fusion(s32[4096]{0:T(1024)S(1)} %get-tuple-element.25, f32[4096,4,2]{0,2,1:T(2,128)S(1)} %convert_bitcast_fusion.2, f32[4096,128]{0,1:T(8,128)S(1)} %convert_bitcast_fusion.1), kind=kOutput, calls=%fused_computation.27 | convolution fusion | flops 1615790080 | bytes 2637824 | tf_op jit(solution)/shard_map/bpi,zi,si->pzbs/dot_general | solution.py:356
  8.9 0.9 fusion.43
  9.8 0.9 fusion.44
  10.7 0.0 copy-done.8
  10.7 0.9 fusion.30
  11.6 0.2 copy.46
  11.7 0.9 fusion.29
  12.6 0.2 copy.45
  12.9 0.8 pad_maximum_fusion
  13.7 6.0 %all-to-all-start = ((bf16[8,208,128]{2,1,0:T(8,128)(2,1)}), bf16[8,208,128]{2,1,0:T(8,128)(2,1)S(1)}, u32[]{:S(2)}, u32[]{:S(2)}) async-start(bf16[8,208,128]{2,1,0:T(8,128)(2,1)} %pad_maximum_fusion), calls=%async_computation | async-start | bytes 851968 | tf_op jit(solution)/shard_map/all_to_all | solution.py:362
  19.6 3.3 %fusion.10 = f32[192,4096]{1,0:T(8,128)} fusion(s32[4096]{0:T(1024)S(1)} %get-tuple-element.25), kind=kOutput, calls=%fused_computation.17 | convolution fusion | flops 303181824 | bytes 3162112 | tf_op jit(solution)/shard_map/zk,ki->zi/dot_general | solution.py:386
  22.9 3.2 %fusion.9 = f32[192,4096]{1,0:T(8,128)} fusion(s32[4096]{0:T(1024)S(1)} %get-tuple-element.25), kind=kOutput, calls=%fused_computation.16 | convolution fusion | flops 303181824 | bytes 3162112 | tf_op jit(solution)/shard_map/zk,ki->zi/dot_general | solution.py:387
  26.2 0.4 fusion.13
  26.6 0.0 copy-done.6
  26.7 0.1 fusion.107
  26.8 0.1 fusion.105
  26.9 0.0 copy-done.5
  26.9 0.2 copy.66
  27.0 0.2 convolution_bitcast_fusion.3
  27.2 0.0 copy-done.7
  27.3 5.1 %copy.47 = f32[24,192,192]{2,0,1:T(8,128)S(1)} copy(f32[24,192,192]{2,1,0:T(8,128)} %param.11) | data formatting | bytes 7077888 | tf_op args[3]
  32.4 0.0 copy-start
  32.4 0.0 copy-start.1
  32.4 4.9 %copy.80 = f32[24,96,2,192]{3,1,2,0:T(8,128)} copy(f32[24,96,2,192]{3,0,2,1:T(8,128)S(1)} %bitcast.109) | data formatting | bytes 7077888 | tf_op jit(solution)/shard_map/reshape | solution.py:260
  37.3 0.0 collective-permute-done
  37.3 0.1 copy.67
  37.4 0.2 convolution_bitcast_fusion.2
  37.6 0.0 collective-permute-done.2
  37.6 0.2 copy.69
  37.8 0.2 convolution_bitcast_fusion
  38.0 0.0 collective-permute-done.1
  38.0 0.2 copy.68
  38.2 0.2 convolution_bitcast_fusion.1
  38.4 0.1 concatenate.38
  38.4 0.1 constant_dynamic-slice_fusion
  38.5 0.1 reshape.137
  38.6 0.1 copy.50
  38.7 0.1 copy.51
  38.8 0.1 fusion.63
  38.9 0.0 all-to-all-done.refs_0_
  38.9 0.0 copy-done
  38.9 0.0 copy-done.1
  38.9 0.0 copy-start.4
  38.9 48.5 %shard_map.95 = bf16[8,192,128]{2,1,0:T(8,128)(2,1)S(1)} custom-call(bf16[8,208,128]{2,1,0:T(8,128)(2,1)S(1)} %all-to-all-done.refs_0_, f32[24,2,96,192]{3,2,1,0:T(8,128)} %bitcast.112, bf16[2,192,512]{2,1,0:T(8,128)(2,1)S(1)} %copy-done.1, bf16[4,192,192]{2,1,0:T(8,128)(2,1)S(1)} %copy-done), custom_call_target="tpu_custom_call" | custom-call | flops 40000000000 | bytes 8000000 | tf_op jit(solution)/shard_map/pallas_call | solution.py:269
  87.5 0.8 pad_maximum_fusion.1
  88.3 6.0 %all-to-all-start.1 = ((bf16[8,208,128]{2,1,0:T(8,128)(2,1)}), bf16[8,208,128]{2,1,0:T(8,128)(2,1)S(1)}, u32[]{:S(2)}, u32[]{:S(2)}) async-start(bf16[8,208,128]{2,1,0:T(8,128)(2,1)} %pad_maximum_fusion.1), calls=%async_computation.1 | async-start | bytes 851968 | tf_op jit(solution)/shard_map/all_to_all | solution.py:374
  94.2 0.0 copy-done.4
  94.3 0.1 fusion.106
  94.4 12.7 %all-to-all-done.1 = bf16[8,208,128]{2,1,0:T(8,128)(2,1)S(1)} async-done(((bf16[8,208,128]{2,1,0:T(8,128)(2,1)}), bf16[8,208,128]{2,1,0:T(8,128)(2,1)S(1)}, u32[]{:S(2)}, u32[]{:S(2)}) %all-to-all-start.1) | async-done | bytes 426016 | tf_op jit(solution)/shard_map/all_to_all | solution.py:374
  107.1 0.1 slice_add_fusion
  107.1 0.1 add.86
  107.2 0.7 copy.59
  107.9 0.0 copy-start.2
  108.0 3.6 %convert_bitcast_fusion = bf16[2,8,24,4,4096]{4,2,3,0,1:T(8,128)(2,1)S(1)} fusion(s32[4096]{0:T(1024)S(1)} %get-tuple-element.24, bf16[8,2,24,4,128]{4,3,2,1,0:T(4,128)(2,1)S(1)} %bitcast.115), kind=kOutput, calls=%fused_computation.11 | convolution fusion | flops 1617428480 | bytes 12992512 | tf_op jit(solution)/shard_map/dpzbs,si->pdzbi/dot_general | solution.py:382
  111.6 4.8 %fusion.4 = (f32[4,4096]{1,0:T(4,128)S(1)}, f32[4,4096]{1,0:T(4,128)S(1)}) fusion(f32[8,24,4096]{2,1,0:T(8,128)S(1)} %bitcast.111, f32[8,24,4096]{2,1,0:T(8,128)S(1)} %bitcast.110, bf16[2,8,24,4,4096]{4,2,3,0,1:T(8,128)(2,1)S(1)} %convert_bitcast_fusion), kind=kLoop, calls=%fused_computation.8 | loop fusion | flops 31424512 | bytes 19005440 | tf_op jit(solution)/shard_map/reduce_sum | solution.py:392
  116.4 0.1 fusion.62
  116.6 0.7 copy.58
  (22 shorter events, 0.3 us)
Async XLA Ops:
  0.6 36.6 %collective-permute-start = (bf16[16,2,4096]{2,1,0:T(2,128)(2,1)}, bf16[16,2,4096]{2,1,0:T(2,128)(2,1)S(1)}, u32[]{:S(2)}, u32[]{:S(2)}) collective-permute-start(bf16[16,2,4096]{2,1,0:T(2,128)(2,1)} %param.12), channel_id=1, source_target_pairs={{8,0},{16,8},{24,16},{0,24},{9,1},{17,9},{25,17},{1,25},{10,2},{18... | collective-permute-start | bytes 786440 | tf_op jit(solution)/shard_map/ppermute | solution.py:299
  3.1 34.5 %collective-permute-start.2 = (bf16[16,2,4096]{2,1,0:T(2,128)(2,1)}, bf16[16,2,4096]{2,1,0:T(2,128)(2,1)S(1)}, u32[]{:S(2)}, u32[]{:S(2)}) collective-permute-start(bf16[16,2,4096]{2,1,0:T(2,128)(2,1)} %param.12), channel_id=1, source_target_pairs={{24,0},{0,8},{8,16},{16,24},{25,1},{1,9},{9,17},{17,25},{26,2},{2,... | collective-permute-start | bytes 786440 | tf_op jit(solution)/shard_map/ppermute | solution.py:299
  3.1 34.9 %collective-permute-start.1 = (bf16[16,2,4096]{2,1,0:T(2,128)(2,1)}, bf16[16,2,4096]{2,1,0:T(2,128)(2,1)S(1)}, u32[]{:S(2)}, u32[]{:S(2)}) collective-permute-start(bf16[16,2,4096]{2,1,0:T(2,128)(2,1)} %param.12), channel_id=1, source_target_pairs={{16,0},{24,8},{0,16},{8,24},{17,1},{25,9},{1,17},{9,25},{18,2},{26... | collective-permute-start | bytes 786440 | tf_op jit(solution)/shard_map/ppermute | solution.py:299
  6.0 4.7 %copy-start.8 = (s32[128]{0:T(128)S(1)}, s32[128]{0:T(128)}, u32[]{:S(2)}) copy-start(s32[128]{0:T(128)} %param.10) | copy-start | bytes 1540
  12.6 14.0 %copy-start.6 = (bf16[4,2,4096]{2,1,0:T(2,128)(2,1)S(1)}, bf16[4,2,4096]{2,1,0:T(2,128)(2,1)}, u32[]{:S(2)}) copy-start(bf16[4,2,4096]{2,1,0:T(2,128)(2,1)} %param.13) | copy-start | bytes 196612
  12.6 14.2 %copy-start.5 = (bf16[16,2,4096]{2,1,0:T(2,128)(2,1)S(1)}, bf16[16,2,4096]{2,1,0:T(2,128)(2,1)}, u32[]{:S(2)}) copy-start(bf16[16,2,4096]{2,1,0:T(2,128)(2,1)} %param.12) | copy-start | bytes 786436
  13.7 13.6 %copy-start.7 = (s32[4096]{0:T(1024)S(1)}, s32[4096]{0:T(1024)}, u32[]{:S(2)}) copy-start(s32[4096]{0:T(1024)} %param.9) | copy-start | bytes 49156
  13.7 25.2 %all-to-all-start = ((bf16[8,208,128]{2,1,0:T(8,128)(2,1)}), bf16[8,208,128]{2,1,0:T(8,128)(2,1)S(1)}, u32[]{:S(2)}, u32[]{:S(2)}) async-start(bf16[8,208,128]{2,1,0:T(8,128)(2,1)} %pad_maximum_fusion), calls=%async_computation | async-start | bytes 851968 | tf_op jit(solution)/shard_map/all_to_all | solution.py:362
  32.4 6.5 %copy-start = (bf16[4,192,192]{2,1,0:T(8,128)(2,1)S(1)}, bf16[4,192,192]{2,1,0:T(8,128)(2,1)}, u32[]{:S(2)}) copy-start(bf16[4,192,192]{2,1,0:T(8,128)(2,1)} %constant.103.clone.refs_3_) | copy-start | bytes 884740
  32.4 6.5 %copy-start.1 = (bf16[2,192,512]{2,1,0:T(8,128)(2,1)S(1)}, bf16[2,192,512]{2,1,0:T(8,128)(2,1)}, u32[]{:S(2)}) copy-start(bf16[2,192,512]{2,1,0:T(8,128)(2,1)} %constant.102.clone.refs_2_) | copy-start | bytes 1179652
  38.9 55.4 %copy-start.4 = (bf16[4,2,4096]{2,1,0:T(2,128)(2,1)S(1)}, bf16[4,2,4096]{2,1,0:T(2,128)(2,1)}, u32[]{:S(2)}) copy-start(bf16[4,2,4096]{2,1,0:T(2,128)(2,1)} %param.8) | copy-start | bytes 196612
  88.3 18.8 %all-to-all-start.1 = ((bf16[8,208,128]{2,1,0:T(8,128)(2,1)}), bf16[8,208,128]{2,1,0:T(8,128)(2,1)S(1)}, u32[]{:S(2)}, u32[]{:S(2)}) async-start(bf16[8,208,128]{2,1,0:T(8,128)(2,1)} %pad_maximum_fusion.1), calls=%async_computation.1 | async-start | bytes 851968 | tf_op jit(solution)/shard_map/all_to_all | solution.py:374
  107.9 3.7 %copy-start.2 = (f32[192,4096]{1,0:T(8,128)S(1)}, f32[192,4096]{1,0:T(8,128)}, u32[]{:S(2)}) copy-start(f32[192,4096]{1,0:T(8,128)} %fusion.10) | copy-start | bytes 9437188
  108.0 3.7 %copy-start.3 = (f32[192,4096]{1,0:T(8,128)S(1)}, f32[192,4096]{1,0:T(8,128)}, u32[]{:S(2)}) copy-start(f32[192,4096]{1,0:T(8,128)} %fusion.9) | copy-start | bytes 9437188
where the time goes:
time: 118 us; the launch traced here: 117 us
  Pallas kernels  48.5 us (41%)
  matrix products  17.9 us (15%)
  starting transfers between devices  15.5 us (13%)
  local copies, waits for them, and re-layouts  13.1 us (11%)
  waiting for transfers between devices  12.7 us (11%)
  other arithmetic  8.67 us (7%)
    pallas_call x1, Pallas kernels, plane_work(): pl.pallas_call(lambda *refs: plane_kernel(slab, *refs), grid=(slab // PLA...  48.5 us
    all_to_all x1, waiting for transfers between devices, fast_device(): lax.all_to_all(jnp.concatenate([planes, both], axis=1), 'fft', split_axis...  12.7 us
    unnamed x28, local copies, waits for them, and re-layouts  7.18 us
    all_to_all x1, starting transfers between devices, fast_device(): lax.all_to_all(jnp.concatenate([planes, both], axis=1), 'fft', split_axis...  6 us
    all_to_all x1, starting transfers between devices, fast_device(): lax.all_to_all(sent, 'fft', split_axis=0, concat_axis=0, tiled=True)  5.97 us
    reshape x1, local copies, waits for them, and re-layouts, plane_work(): potential.reshape(slab, size // 2, 2, size).transpose(0, 2, 1, 3)  4.87 us
    reduce_sum x1, other arithmetic, fast_device(): wave_real = jnp.sum(pick_real * cosine_cols - pick_imag * sine_cols, axis=0)  4.76 us
    dot_general x1, matrix products, fast_device(): jnp.einsum('dpzbs,si->pdzbi', stick_values, stick_hot, preferred_element_...  3.65 us
  transfers between devices with their start and end apart: 5, of which 1 were waited for; matrix products, arithmetic and copies ran while one was open for 24% of the time, Pallas kernels for 0%

commit v1 on v0

--- a/solution.py
+++ b/solution.py
@@ -130,6 +130,7 @@
 
 PLANES = 4
 EXTRA = 16
+LANES = 128
 
 
 def phases(products, length):
@@ -157,16 +158,32 @@
 
 
 def plane_kernel(
-    slab, stick_ref, pot_ref, line_ref, half_ref, out_ref, rows_ref, real_ref, imag_ref
+    slab,
+    stick_ref,
+    pot_ref,
+    line_ref,
+    half_ref,
+    extra_ref,
+    back_ref,
+    rows_ref,
+    real_ref,
+    imag_ref,
+    after_real_ref,
+    after_imag_ref,
+    left_ref,
+    right_ref,
+    stage_ref,
+    send_sem,
+    recv_sem,
 ):
-    group = pl.program_id(0)
     owners, _, sticks = stick_ref.shape
     lines, size, _ = real_ref.shape
     half = size // 2
     wide = line_ref.shape[2] // 2
-    part_rows = out_ref.shape[1] // 2
-    first = pl.multiple_of(group * lines, lines)
-    second = pl.multiple_of(part_rows + group * lines, lines)
+    groups = slab // PLANES
+    part_rows = groups * lines
+    me = lax.axis_index("fft")
+    others = [lax.rem(me + shift, owners) for shift in range(1, owners)]
     scale = 1.0 / (size * size)
 
     def stick_mask(owner):
@@ -174,121 +191,187 @@
         local = lax.broadcasted_iota(jnp.int32, (slab, sticks), 0).astype(jnp.float32)
         return coords[0:1, :] == local
 
-    @pl.when(group == 0)
-    def _():
-        @pl.loop(0, owners)
+    def plane_group(group):
+        first = pl.multiple_of(group * lines, lines)
+        second = pl.multiple_of(part_rows + group * lines, lines)
+
+        @pl.loop(0, owners, unroll=2)
         def _(owner):
-            coords = stick_ref[owner, 2 * part_rows : 2 * part_rows + EXTRA, :].astype(jnp.float32)
-            cells = lax.broadcasted_iota(jnp.int32, (size, sticks), 0).astype(jnp.float32)
-            hot = jnp.where(coords[1:2, :] == cells, 1.0, 0.0).astype(jnp.bfloat16)
-            for part in range(2):
-                rows = lax.dot_general(
-                    hot, line_ref[part], (((0,), (0,)), ((), ())),
+            mask = stick_mask(owner)[None]
+            spread = []
+            for start in (first, second):
+                values = stick_ref[owner, pl.ds(start, lines), :].astype(jnp.float32)
+                spread.append(
+                    jnp.where(mask, values[:, None, :], 0.0).reshape(lines * slab, sticks)
+                )
+            left = jnp.concatenate(spread, axis=1).astype(jnp.bfloat16)
+            result = jnp.dot(left, rows_ref[owner], preferred_element_type=jnp.float32)
+            place = pl.ds(pl.multiple_of(owner * slab, 8), slab)
+            real_ref[:, place, :] = result[:, :size].reshape(lines, slab, size)
+            imag_ref[:, place, :] = result[:, wide : wide + size].reshape(lines, slab, size)
+
+        def one_plane(line, plane):
+            real_low, real_high = real_ref[line, :half, :], real_ref[line, half:, :]
+            imag_low, imag_high = imag_ref[line, :half, :], imag_ref[line, half:, :]
+            total = jnp.concatenate([real_low + real_high, imag_low + imag_high], axis=0)
+            differ = jnp.concatenate([real_low - real_high, imag_low - imag_high], axis=0)
+
+            def there_and_back(values, parity):
+                forward = jnp.dot(
+                    half_ref[parity],
+                    values.astype(jnp.bfloat16),
                     preferred_element_type=jnp.float32,
                 )
-                rows_ref[owner, part * sticks : (part + 1) * sticks, :] = rows.astype(jnp.bfloat16)
+                picks = pl.ds(parity, half, 2)
+                local = jnp.concatenate(
+                    [left_ref[plane, picks, :], right_ref[plane, picks, :][:, : size - LANES]], axis=1
+                )
+                weighted = jnp.concatenate([forward[:half] * local, forward[half:] * local], axis=0)
+                return jnp.dot(
+                    half_ref[2 + parity],
+                    weighted.astype(jnp.bfloat16),
+                    preferred_element_type=jnp.float32,
+                )
+
+            even = there_and_back(total, 0)
+            odd = there_and_back(differ, 1)
+            low, high = even + odd, even - odd
+            after_real_ref[line, :half, :] = low[:half]
+            after_imag_ref[line, :half, :] = low[half:]
+            after_real_ref[line, half:, :] = high[:half]
+            after_imag_ref[line, half:, :] = high[half:]
+
+        bands = lines // PLANES
+
+        @pl.loop(0, PLANES)
+        def _(plane):
+            whole_plane = group * PLANES + plane
+            left_ref[plane] = pot_ref[whole_plane, :, :LANES]
+            right_ref[plane, :, : size - LANES] = pot_ref[whole_plane, :, LANES:]
+            for band in range(bands):
+                one_plane(plane * bands + band, plane)
+
+        @pl.loop(0, owners, unroll=2)
+        def _(owner):
+            mask = stick_mask(owner)[None]
+            place = pl.ds(pl.multiple_of(owner * slab, 8), slab)
+            real = after_real_ref[:, place, :].reshape(lines * slab, size).astype(jnp.bfloat16)
+            imag = after_imag_ref[:, place, :].reshape(lines * slab, size).astype(jnp.bfloat16)
+            across = (((1,), (1,)), ((), ()))
+            result = lax.dot_general(
+                real, rows_ref[owner, :, :size], across, preferred_element_type=jnp.float32
+            ) + lax.dot_general(
+                imag,
+                rows_ref[owner, :, wide : wide + size],
+                across,
+                preferred_element_type=jnp.float32,
+            )
+            result = result.reshape(lines, slab, 2 * sticks)
+            for part in range(2):
+                chosen = result[:, :, part * sticks : (part + 1) * sticks]
+                picked = jnp.sum(jnp.where(mask, chosen, 0.0), axis=1) * scale
+                start = pl.multiple_of((2 * group + part) * lines, lines)
+                stage_ref[owner, pl.ds(start, lines), :] = picked.astype(jnp.bfloat16)
+
+    def rows_of(group):
+        return pl.ds(pl.multiple_of(group * 2 * lines, 2 * lines), 2 * lines)
+
+    def group_copy(group, place):
+        return pltpu.make_async_remote_copy(
+            src_ref=stage_ref.at[others[place], rows_of(group)],
+            dst_ref=back_ref.at[me, rows_of(group)],
+            send_sem=send_sem.at[group, place],
+            recv_sem=recv_sem.at[group, place],
+            device_id={"fft": others[place]},
+            device_id_type=pl.DeviceIdType.MESH,
+        )
+
+    def extra_copy(place):
+        return pltpu.make_async_remote_copy(
+            src_ref=extra_ref.at[others[place]],
+            dst_ref=back_ref.at[me, pl.ds(2 * part_rows, EXTRA)],
+            send_sem=send_sem.at[groups, place],
+            recv_sem=recv_sem.at[groups, place],
+            device_id={"fft": others[place]},
+            device_id_type=pl.DeviceIdType.MESH,
+        )
+
+    barrier = pltpu.get_barrier_semaphore()
+    for other in others:
+        pl.semaphore_signal(
+            barrier, inc=1, device_id={"fft": other}, device_id_type=pl.DeviceIdType.MESH
+        )
 
     @pl.loop(0, owners)
     def _(owner):
-        mask = stick_mask(owner)[None]
-        spread = []
-        for start in (first, second):
-            values = stick_ref[owner, pl.ds(start, lines), :].astype(jnp.float32)
-            spread.append(jnp.where(mask, values[:, None, :], 0.0).reshape(lines * slab, sticks))
-        left = jnp.concatenate(spread, axis=1).astype(jnp.bfloat16)
-        result = jnp.dot(left, rows_ref[owner], preferred_element_type=jnp.float32)
-        place = pl.ds(pl.multiple_of(owner * slab, 8), slab)
-        real_ref[:, place, :] = result[:, :size].reshape(lines, slab, size)
-        imag_ref[:, place, :] = result[:, wide : wide + size].reshape(lines, slab, size)
-
-    def one_plane(line, plane):
-        real_low, real_high = real_ref[line, :half, :], real_ref[line, half:, :]
-        imag_low, imag_high = imag_ref[line, :half, :], imag_ref[line, half:, :]
-        total = jnp.concatenate([real_low + real_high, imag_low + imag_high], axis=0)
-        differ = jnp.concatenate([real_low - real_high, imag_low - imag_high], axis=0)
-
-        def there_and_back(values, parity):
-            forward = jnp.dot(
-                half_ref[parity], values.astype(jnp.bfloat16), preferred_element_type=jnp.float32
-            )
-            local = pot_ref[plane, parity]
-            weighted = jnp.concatenate([forward[:half] * local, forward[half:] * local], axis=0)
-            return jnp.dot(
-                half_ref[2 + parity],
-                weighted.astype(jnp.bfloat16),
+        coords = stick_ref[owner, 2 * part_rows : 2 * part_rows + EXTRA, :].astype(jnp.float32)
+        cells = lax.broadcasted_iota(jnp.int32, (size, sticks), 0).astype(jnp.float32)
+        hot = jnp.where(coords[1:2, :] == cells, 1.0, 0.0).astype(jnp.bfloat16)
+        for part in range(2):
+            rows = lax.dot_general(
+                hot,
+                line_ref[part],
+                (((0,), (0,)), ((), ())),
                 preferred_element_type=jnp.float32,
             )
-
-        even = there_and_back(total, 0)
-        odd = there_and_back(differ, 1)
-        low, high = even + odd, even - odd
-        real_ref[line, :half, :] = low[:half]
-        imag_ref[line, :half, :] = low[half:]
-        real_ref[line, half:, :] = high[:half]
-        imag_ref[line, half:, :] = high[half:]
-
-    bands = lines // PLANES
-
-    @pl.loop(0, PLANES)
-    def _(plane):
-        for band in range(bands):
-            one_plane(plane * bands + band, plane)
-
-    @pl.loop(0, owners)
-    def _(owner):
-        mask = stick_mask(owner)[None]
-        place = pl.ds(pl.multiple_of(owner * slab, 8), slab)
-        real = real_ref[:, place, :].reshape(lines * slab, size).astype(jnp.bfloat16)
-        imag = imag_ref[:, place, :].reshape(lines * slab, size).astype(jnp.bfloat16)
-        across = (((1,), (1,)), ((), ()))
-        result = lax.dot_general(
-            real, rows_ref[owner, :, :size], across, preferred_element_type=jnp.float32
-        ) + lax.dot_general(
-            imag, rows_ref[owner, :, wide : wide + size], across, preferred_element_type=jnp.float32
-        )
-        result = result.reshape(lines, slab, 2 * sticks)
-        for part, start in enumerate((first, second)):
-            chosen = result[:, :, part * sticks : (part + 1) * sticks]
-            picked = jnp.sum(jnp.where(mask, chosen, 0.0), axis=1) * scale
-            out_ref[owner, pl.ds(start, lines), :] = picked.astype(jnp.bfloat16)
-
-
-def plane_work(received, potential, bands):
+            rows_ref[owner, part * sticks : (part + 1) * sticks, :] = rows.astype(jnp.bfloat16)
+
+    pl.semaphore_wait(barrier, owners - 1)
+    for place in range(owners - 1):
+        extra_copy(place).start()
+
+    @pl.loop(0, groups)
+    def _(group):
+        plane_group(group)
+        for place in range(owners - 1):
+            group_copy(group, place).start()
+
+    back_ref[me, : 2 * part_rows, :] = stage_ref[me]
+    back_ref[me, 2 * part_rows :, :] = extra_ref[me]
+    for place in range(owners - 1):
+        extra_copy(place).wait()
+
+    @pl.loop(0, groups)
+    def _(group):
+        for place in range(owners - 1):
+            group_copy(group, place).wait()
+
+
+def plane_work(received, potential, extra, bands):
     owners, _, sticks = received.shape
     slab, size, _ = potential.shape
     lines = PLANES * bands
-    split_pot = potential.reshape(slab, size // 2, 2, size).transpose(0, 2, 1, 3)
+    groups = slab // PLANES
     lines_table = line_tables(size)
     halves = half_tables(size)
     wide = lines_table.shape[2]
-
-    def whole(array):
-        return pl.BlockSpec(array.shape, lambda g: (0,) * array.ndim)
-
     rows = 2 * slab * bands
+    in_vmem = pl.BlockSpec(memory_space=pltpu.VMEM)
+    grid_part = pltpu.VMEM((lines, size, size), jnp.float32)
     return pl.pallas_call(
-        lambda *refs: plane_kernel(slab, *refs),
-        grid=(slab // PLANES,),
-        out_shape=jax.ShapeDtypeStruct((owners, rows, sticks), jnp.bfloat16),
-        in_specs=[
-            whole(received),
-            pl.BlockSpec((PLANES, 2, size // 2, size), lambda g: (g, 0, 0, 0)),
-            whole(lines_table),
-            whole(halves),
-        ],
-        out_specs=pl.BlockSpec((owners, rows, sticks), lambda g: (0, 0, 0)),
+        functools.partial(plane_kernel, slab),
+        out_shape=jax.ShapeDtypeStruct((owners, rows + EXTRA, sticks), jnp.bfloat16),
+        in_specs=[in_vmem] * 5,
+        out_specs=in_vmem,
         scratch_shapes=[
             pltpu.VMEM((owners, 2 * sticks, wide), jnp.bfloat16),
-            pltpu.VMEM((lines, size, size), jnp.float32),
-            pltpu.VMEM((lines, size, size), jnp.float32),
+            grid_part,
+            grid_part,
+            grid_part,
+            grid_part,
+            pltpu.VMEM((PLANES, size, LANES), jnp.float32),
+            pltpu.VMEM((PLANES, size, LANES), jnp.float32),
+            pltpu.VMEM((owners, rows, sticks), jnp.bfloat16),
+            pltpu.SemaphoreType.DMA((groups + 1, owners - 1)),
+            pltpu.SemaphoreType.DMA((groups + 1, owners - 1)),
         ],
         compiler_params=pltpu.CompilerParams(
-            dimension_semantics=("arbitrary",), vmem_limit_bytes=48 * 1024 * 1024
+            collective_id=0, has_side_effects=True, vmem_limit_bytes=48 * 1024 * 1024
         ),
         cost_estimate=pl.CostEstimate(
             flops=40 * 10**9, bytes_accessed=8 * 10**6, transcendentals=0
         ),
-    )(received, split_pot, lines_table, halves)
+    )(received, potential, lines_table, halves, extra)
 
 
 def gathered_bands(array, mesh_bands):
@@ -360,7 +443,6 @@
     pieces = [part.astype(jnp.bfloat16).reshape(owners, -1, stick_count) for part in along_z]
     sent = jnp.concatenate(pieces + [coords], axis=1)
     received = lax.all_to_all(sent, "fft", split_axis=0, concat_axis=0, tiled=True)
-    planes = plane_work(received, potential, bands)
     split = overlaps(subspace, previous, mesh_bands, owners)
     flat = split.reshape(owners, 1, -1)
     high = lax.reduce_precision(flat, 8, 7)
@@ -371,16 +453,14 @@
     both = jnp.pad(both, ((0, 0), (0, 0), (0, lanes - width)))
     both = both.reshape(owners, -1, stick_count)
     both = jnp.pad(both, ((0, 0), (0, EXTRA - both.shape[1]), (0, 0)))
-    returned = lax.all_to_all(
-        jnp.concatenate([planes, both], axis=1), "fft", split_axis=0, concat_axis=0, tiled=True
-    )
-    rows = planes.shape[1]
+    returned = plane_work(received, potential, both, bands)
+    rows = 2 * slab_depth * bands
     sums = returned[:, rows:].reshape(owners, -1)[:, :width].astype(jnp.float32)
     sums = jnp.sum(sums, axis=0)
     intersection = (sums[: width // 2] + sums[width // 2 :]).reshape(split.shape[1:])
-    stick_values = returned[:, :rows].reshape(owners, 2, slab_depth, bands, stick_count)
+    stick_values = returned[:, :rows].reshape(owners, -1, 2, PLANES, bands, stick_count)
     picked = jnp.einsum(
-        "dpzbs,si->pdzbi", stick_values, stick_hot, preferred_element_type=jnp.float32
+        "dgpzbs,si->pdgzbi", stick_values, stick_hot, preferred_element_type=jnp.float32
     ).astype(jnp.bfloat16)
     picked = picked.reshape(2, grid_size, bands, -1)
     cosine_cols = jnp.einsum("zk,ki->zi", inverse[0], plane_hot, preferred_element_type=jnp.float32)
@@ -402,6 +482,7 @@
     slab_depth = potential.shape[0]
     bands = orbitals.shape[0]
     aligned = slab_depth % 8 == 0 and slab_depth % PLANES == 0
+    aligned = aligned and LANES < potential.shape[1] <= 2 * LANES
     if aligned and PLANES * bands % 16 == 0 and arrays[2].shape[0] % 128 == 0:
         return fast_device(mesh_bands, *arrays)
     return general_device(*arrays)

time: 118 us -> 109 us (0.924)
  waiting for transfers between devices: 12.7 us -> 0.01 us
  local copies, waits for them, and re-layouts: 13.1 us -> 23.6 us
  starting transfers between devices: 15.5 us -> 9.36 us
    mul x0 -> x4, local copies, waits for them, and re-layouts: none -> 20.5 us  [fast_device(): wave_real = jnp.sum(pick_real * cosine_cols - pick_imag * sine_cols, axis=0)]
    all_to_all x1 -> x0, waiting for transfers between devices: 12.7 us -> none  [fast_device(): lax.all_to_all(jnp.concatenate([planes, both], axis=1), 'fft', split_axis...]
    all_to_all x1 -> x0, starting transfers between devices: 6 us -> none  [fast_device(): lax.all_to_all(jnp.concatenate([planes, both], axis=1), 'fft', split_axis...]
    unnamed x28 -> x27, local copies, waits for them, and re-layouts: 7.18 us -> 2.11 us
    reshape x1 -> x0, local copies, waits for them, and re-layouts: 4.87 us -> none  [plane_work(): potential.reshape(slab, size // 2, 2, size).transpose(0, 2, 1, 3)]
  transfers between devices with their start and end apart: 5 -> 4, of which waited for: 1 -> 0; matrix products, arithmetic and copies ran while one was open for 24% -> 36% of each run, Pallas kernels for 0% -> 0%
where the time goes in v1:
time: 109 us
  Pallas kernels  49.1 us (45%)
  local copies, waits for them, and re-layouts  23.6 us (22%)
  matrix products  17.8 us (16%)
  starting transfers between devices  9.36 us (9%)
  other arithmetic  7.88 us (7%)
    pallas_call x1, Pallas kernels, plane_work(): pl.pallas_call(functools.partial(plane_kernel, slab), out_shape=jax.Shape...  49.1 us
    mul x4, local copies, waits for them, and re-layouts, fast_device(): wave_real = jnp.sum(pick_real * cosine_cols - pick_imag * sine_cols, axis=0)  20.5 us
    all_to_all x1, starting transfers between devices, fast_device(): lax.all_to_all(sent, 'fft', split_axis=0, concat_axis=0, tiled=True)  5.84 us
    reduce_sum x1, other arithmetic, fast_device(): wave_real = jnp.sum(pick_real * cosine_cols - pick_imag * sine_cols, axis=0)  4.76 us
    dot_general x1, matrix products, fast_device(): jnp.einsum('dgpzbs,si->pdgzbi', stick_values, stick_hot, preferred_elemen...  3.62 us
    dot_general x4, matrix products, product(): jnp.einsum(form, operand, table_part, preferred_element_type=jnp.float32)  3.56 us
    ppermute x3, starting transfers between devices, gathered_bands(): blocks.append(lax.ppermute(array, 'band', pairs))  3.53 us
    dot_general x1, matrix products, fast_device(): jnp.einsum('zk,ki->zi', inverse[1], plane_hot, preferred_element_type=jnp...  3.29 us
  transfers between devices with their start and end apart: 4, of which 0 were waited for; matrix products, arithmetic and copies ran while one was open for 36% of the time, Pallas kernels for 0%

profile of v1, /device:TPU:0, one launch (start us, length us, event | category | flops | bytes accessed | tf_op | source)
XLA Modules:
  0.0 108.7 jit_solution(9260404845497131965)
XLA Ops:
  0.6 2.5 %collective-permute-start = (bf16[16,2,4096]{2,1,0:T(2,128)(2,1)}, bf16[16,2,4096]{2,1,0:T(2,128)(2,1)S(1)}, u32[]{:S(2)}, u32[]{:S(2)}) collective-permute-start(bf16[16,2,4096]{2,1,0:T(2,128)(2,1)} %param.12), channel_id=1, source_target_pairs={{8,0},{16,8},{24,16},{0,24},{9,1},{17,9},{25,17},{1,25},{10,2},{18... | collective-permute-start | bytes 786440 | tf_op jit(solution)/shard_map/ppermute | solution.py:382
  3.1 0.0 collective-permute-start.2
  3.1 1.1 collective-permute-start.1
  4.2 0.7 add_select_fusion.2
  4.9 0.9 convert_bitcast_fusion.2
  5.8 0.2 convert_bitcast_fusion.1
  6.0 0.0 copy-start.8
  6.0 2.9 %fusion.24 = bf16[2,192,4,128]{3,1,0,2:T(8,128)(2,1)S(1)} fusion(s32[4096]{0:T(1024)S(1)} %get-tuple-element.25, f32[4096,4,2]{0,2,1:T(2,128)S(1)} %convert_bitcast_fusion.2, f32[4096,128]{0,1:T(8,128)S(1)} %convert_bitcast_fusion.1), kind=kOutput, calls=%fused_computation.26 | convolution fusion | flops 1615790080 | bytes 2637824 | tf_op jit(solution)/shard_map/bpi,zi,si->pzbs/dot_general | solution.py:439
  8.9 0.0 copy-start.4
  8.9 0.9 fusion.43
  9.8 0.9 fusion.44
  10.7 0.0 copy-done.8
  10.7 0.9 fusion.30
  11.6 0.2 copy.48
  11.8 0.9 fusion.29
  12.7 0.2 copy.47
  12.9 0.8 pad_maximum_fusion
  13.7 5.8 %all-to-all-start = ((bf16[8,208,128]{2,1,0:T(8,128)(2,1)}), bf16[8,208,128]{2,1,0:T(8,128)(2,1)S(1)}, u32[]{:S(2)}, u32[]{:S(2)}) async-start(bf16[8,208,128]{2,1,0:T(8,128)(2,1)} %pad_maximum_fusion), calls=%async_computation | async-start | bytes 851968 | tf_op jit(solution)/shard_map/all_to_all | solution.py:445
  19.5 0.0 copy-done.4
  19.5 0.1 fusion.106
  19.6 0.0 copy-start.6
  19.6 0.0 copy-start.5
  19.6 3.2 %fusion.10 = f32[192,4096]{1,0:T(8,128)} fusion(s32[4096]{0:T(1024)S(1)} %get-tuple-element.25), kind=kOutput, calls=%fused_computation.16 | convolution fusion | flops 303181824 | bytes 3162112 | tf_op jit(solution)/shard_map/zk,ki->zi/dot_general | solution.py:466
  22.9 3.3 %fusion.9 = f32[192,4096]{1,0:T(8,128)} fusion(s32[4096]{0:T(1024)S(1)} %get-tuple-element.25), kind=kOutput, calls=%fused_computation.15 | convolution fusion | flops 303181824 | bytes 3162112 | tf_op jit(solution)/shard_map/zk,ki->zi/dot_general | solution.py:467
  26.1 0.4 fusion.13
  26.6 0.0 copy-done.6
  26.6 0.1 fusion.107
  26.8 0.1 fusion.105
  26.8 0.0 copy-done.5
  26.8 0.2 copy.68
  27.0 0.2 convolution_bitcast_fusion.3
  27.2 0.0 copy-done.7
  27.3 4.9 %mul.157 = f32[8,6,4,4096]{3,2,1,0:T(4,128)} reshape(f32[192,4096]{1,0:T(8,128)} %fusion.10) | data formatting | bytes 6291456 | tf_op jit(solution)/shard_map/mul | solution.py:472
  32.2 5.3 %copy.56 = f32[8,6,4,4096]{3,0,2,1:T(8,128)} copy(f32[8,6,4,4096]{3,2,1,0:T(4,128)} %mul.157) | data formatting | bytes 6291456 | tf_op jit(solution)/shard_map/mul | solution.py:472
  37.5 4.9 %mul.162 = f32[8,6,4,4096]{3,2,1,0:T(4,128)} reshape(f32[192,4096]{1,0:T(8,128)} %fusion.9) | data formatting | bytes 6291456 | tf_op jit(solution)/shard_map/mul | solution.py:472
  42.4 5.4 %copy.57 = f32[8,6,4,4096]{3,0,2,1:T(8,128)} copy(f32[8,6,4,4096]{3,2,1,0:T(4,128)} %mul.162) | data formatting | bytes 6291456 | tf_op jit(solution)/shard_map/mul | solution.py:472
  47.7 0.0 collective-permute-done
  47.7 0.1 copy.69
  47.9 0.2 convolution_bitcast_fusion.2
  48.1 0.0 collective-permute-done.2
  48.1 0.2 copy.71
  48.2 0.2 convolution_bitcast_fusion
  48.4 0.0 collective-permute-done.1
  48.4 0.2 copy.70
  48.6 0.2 convolution_bitcast_fusion.1
  48.8 0.1 concatenate.35
  48.9 0.1 constant_dynamic-slice_fusion
  49.0 0.1 reshape.133
  49.0 0.1 copy.50
  49.1 0.1 copy.51
  49.2 0.1 fusion.63.extra_ref
  49.3 0.0 all-to-all-done.stick_ref
  49.3 0.0 copy-done
  49.3 0.0 copy-done.1
  49.3 49.1 %shard_map.95 = bf16[8,208,128]{2,1,0:T(8,128)(2,1)S(1)} custom-call(bf16[8,208,128]{2,1,0:T(8,128)(2,1)S(1)} %all-to-all-done.stick_ref, f32[24,192,192]{2,1,0:T(8,128)} %pot_ref.1, bf16[2,192,512]{2,1,0:T(8,128)(2,1)S(1)} %copy-done.1, bf16[4,192,192]{2,1,0:T(8,128)(2,1)S(1)} %copy-done, bf16[8,16,128]{2,1,0:T(8,128)(2,1)S(1)} %fusion.63.extra_ref), custom_call_target="tpu_custom_call" | custom-call | flops 40000000000 | bytes 8000000 | tf_op jit(solution)/shard_map/pallas_call | solution.py:351
  98.5 0.1 slice_add_fusion
  98.6 0.1 add.86
  98.7 0.7 copy.61
  99.4 3.6 %convert_bitcast_fusion = bf16[2,8,6,4,4,4096]{5,1,4,3,0,2:T(8,128)(2,1)S(1)} fusion(s32[4096]{0:T(1024)S(1)} %get-tuple-element.24, bf16[8,6,2,4,4,128]{5,4,3,2,1,0:T(4,128)(2,1)S(1)} %bitcast.105), kind=kOutput, calls=%fused_computation.11 | convolution fusion | flops 1617428480 | bytes 12992512 | tf_op jit(solution)/shard_map/dgpzbs,si->pdgzbi/dot_general | solution.py:462
  103.0 0.0 copy-done.2
  103.0 0.0 copy-done.3
  103.0 4.8 %fusion.4 = (f32[4,4096]{1,0:T(4,128)S(1)}, f32[4,4096]{1,0:T(4,128)S(1)}) fusion(f32[8,6,4,4096]{3,0,2,1:T(8,128)S(1)} %copy-done.3, f32[8,6,4,4096]{3,0,2,1:T(8,128)S(1)} %copy-done.2, bf16[2,8,6,4,4,4096]{5,1,4,3,0,2:T(8,128)(2,1)S(1)} %convert_bitcast_fusion), kind=kLoop, calls=%fused_computation.8 | loop fusion | flops 31424512 | bytes 19005440 | tf_op jit(solution)/shard_map/reduce_sum | solution.py:472
  107.8 0.1 fusion.62
  108.0 0.7 copy.60
  (21 shorter events, 0.3 us)
Async XLA Ops:
  0.6 47.1 %collective-permute-start = (bf16[16,2,4096]{2,1,0:T(2,128)(2,1)}, bf16[16,2,4096]{2,1,0:T(2,128)(2,1)S(1)}, u32[]{:S(2)}, u32[]{:S(2)}) collective-permute-start(bf16[16,2,4096]{2,1,0:T(2,128)(2,1)} %param.12), channel_id=1, source_target_pairs={{8,0},{16,8},{24,16},{0,24},{9,1},{17,9},{25,17},{1,25},{10,2},{18... | collective-permute-start | bytes 786440 | tf_op jit(solution)/shard_map/ppermute | solution.py:382
  3.1 45.0 %collective-permute-start.2 = (bf16[16,2,4096]{2,1,0:T(2,128)(2,1)}, bf16[16,2,4096]{2,1,0:T(2,128)(2,1)S(1)}, u32[]{:S(2)}, u32[]{:S(2)}) collective-permute-start(bf16[16,2,4096]{2,1,0:T(2,128)(2,1)} %param.12), channel_id=1, source_target_pairs={{24,0},{0,8},{8,16},{16,24},{25,1},{1,9},{9,17},{17,25},{26,2},{2,... | collective-permute-start | bytes 786440 | tf_op jit(solution)/shard_map/ppermute | solution.py:382
  3.1 45.4 %collective-permute-start.1 = (bf16[16,2,4096]{2,1,0:T(2,128)(2,1)}, bf16[16,2,4096]{2,1,0:T(2,128)(2,1)S(1)}, u32[]{:S(2)}, u32[]{:S(2)}) collective-permute-start(bf16[16,2,4096]{2,1,0:T(2,128)(2,1)} %param.12), channel_id=1, source_target_pairs={{16,0},{24,8},{0,16},{8,24},{17,1},{25,9},{1,17},{9,25},{18,2},{26... | collective-permute-start | bytes 786440 | tf_op jit(solution)/shard_map/ppermute | solution.py:382
  6.0 4.7 %copy-start.8 = (s32[128]{0:T(128)S(1)}, s32[128]{0:T(128)}, u32[]{:S(2)}) copy-start(s32[128]{0:T(128)} %param.10) | copy-start | bytes 1540
  8.9 10.6 %copy-start.4 = (bf16[4,2,4096]{2,1,0:T(2,128)(2,1)S(1)}, bf16[4,2,4096]{2,1,0:T(2,128)(2,1)}, u32[]{:S(2)}) copy-start(bf16[4,2,4096]{2,1,0:T(2,128)(2,1)} %param.8) | copy-start | bytes 196612
  13.7 35.7 %all-to-all-start = ((bf16[8,208,128]{2,1,0:T(8,128)(2,1)}), bf16[8,208,128]{2,1,0:T(8,128)(2,1)S(1)}, u32[]{:S(2)}, u32[]{:S(2)}) async-start(bf16[8,208,128]{2,1,0:T(8,128)(2,1)} %pad_maximum_fusion), calls=%async_computation | async-start | bytes 851968 | tf_op jit(solution)/shard_map/all_to_all | solution.py:445
  19.6 7.0 %copy-start.6 = (bf16[4,2,4096]{2,1,0:T(2,128)(2,1)S(1)}, bf16[4,2,4096]{2,1,0:T(2,128)(2,1)}, u32[]{:S(2)}) copy-start(bf16[4,2,4096]{2,1,0:T(2,128)(2,1)} %param.13) | copy-start | bytes 196612
  19.6 7.2 %copy-start.5 = (bf16[16,2,4096]{2,1,0:T(2,128)(2,1)S(1)}, bf16[16,2,4096]{2,1,0:T(2,128)(2,1)}, u32[]{:S(2)}) copy-start(bf16[16,2,4096]{2,1,0:T(2,128)(2,1)} %param.12) | copy-start | bytes 786436
  22.9 4.4 %copy-start.7 = (s32[4096]{0:T(1024)S(1)}, s32[4096]{0:T(1024)}, u32[]{:S(2)}) copy-start(s32[4096]{0:T(1024)} %param.9) | copy-start | bytes 49156
  47.7 1.6 %copy-start = (bf16[4,192,192]{2,1,0:T(8,128)(2,1)S(1)}, bf16[4,192,192]{2,1,0:T(8,128)(2,1)}, u32[]{:S(2)}) copy-start(bf16[4,192,192]{2,1,0:T(8,128)(2,1)} %constant.103.clone.half_ref) | copy-start | bytes 884740
  47.7 1.6 %copy-start.1 = (bf16[2,192,512]{2,1,0:T(8,128)(2,1)S(1)}, bf16[2,192,512]{2,1,0:T(8,128)(2,1)}, u32[]{:S(2)}) copy-start(bf16[2,192,512]{2,1,0:T(8,128)(2,1)} %constant.102.clone.line_ref) | copy-start | bytes 1179652
  99.4 3.6 %copy-start.2 = (f32[8,6,4,4096]{3,0,2,1:T(8,128)S(1)}, f32[8,6,4,4096]{3,0,2,1:T(8,128)}, u32[]{:S(2)}) copy-start(f32[8,6,4,4096]{3,0,2,1:T(8,128)} %copy.56) | copy-start | bytes 9437188
  99.4 3.6 %copy-start.3 = (f32[8,6,4,4096]{3,0,2,1:T(8,128)S(1)}, f32[8,6,4,4096]{3,0,2,1:T(8,128)}, u32[]{:S(2)}) copy-start(f32[8,6,4,4096]{3,0,2,1:T(8,128)} %copy.57) | copy-start | bytes 9437188

commit v2 on v1

--- a/solution.py
+++ b/solution.py
@@ -157,14 +157,21 @@
     return jnp.asarray(np.stack(tables), jnp.bfloat16)
 
 
+def column_tables(length):
+    cosine, sine = phases(np.outer(np.arange(length), np.arange(length)), length)
+    there = np.block([[cosine, -sine], [sine, cosine]])
+    return jnp.asarray(there, jnp.bfloat16), jnp.asarray(there.T, jnp.bfloat16)
+
+
 def plane_kernel(
     slab,
-    stick_ref,
+    sent_ref,
     pot_ref,
     line_ref,
     half_ref,
     extra_ref,
     back_ref,
+    stick_ref,
     rows_ref,
     real_ref,
     imag_ref,
@@ -176,7 +183,7 @@
     send_sem,
     recv_sem,
 ):
-    owners, _, sticks = stick_ref.shape
+    owners, _, sticks = sent_ref.shape
     lines, size, _ = real_ref.shape
     half = size // 2
     wide = line_ref.shape[2] // 2
@@ -296,11 +303,30 @@
             device_id_type=pl.DeviceIdType.MESH,
         )
 
+    def stick_copy(place):
+        return pltpu.make_async_remote_copy(
+            src_ref=sent_ref.at[others[place]],
+            dst_ref=stick_ref.at[me],
+            send_sem=send_sem.at[groups + 1, place],
+            recv_sem=recv_sem.at[groups + 1, place],
+            device_id={"fft": others[place]},
+            device_id_type=pl.DeviceIdType.MESH,
+        )
+
     barrier = pltpu.get_barrier_semaphore()
     for other in others:
         pl.semaphore_signal(
             barrier, inc=1, device_id={"fft": other}, device_id_type=pl.DeviceIdType.MESH
         )
+
+    pl.semaphore_wait(barrier, owners - 1)
+    for place in range(owners - 1):
+        stick_copy(place).start()
+    for place in range(owners - 1):
+        extra_copy(place).start()
+    stick_ref[me] = sent_ref[me]
+    for place in range(owners - 1):
+        stick_copy(place).wait()
 
     @pl.loop(0, owners)
     def _(owner):
@@ -316,10 +342,6 @@
             )
             rows_ref[owner, part * sticks : (part + 1) * sticks, :] = rows.astype(jnp.bfloat16)
 
-    pl.semaphore_wait(barrier, owners - 1)
-    for place in range(owners - 1):
-        extra_copy(place).start()
-
     @pl.loop(0, groups)
     def _(group):
         plane_group(group)
@@ -337,8 +359,8 @@
             group_copy(group, place).wait()
 
 
-def plane_work(received, potential, extra, bands):
-    owners, _, sticks = received.shape
+def plane_work(sent, potential, extra, bands):
+    owners, _, sticks = sent.shape
     slab, size, _ = potential.shape
     lines = PLANES * bands
     groups = slab // PLANES
@@ -354,6 +376,7 @@
         in_specs=[in_vmem] * 5,
         out_specs=in_vmem,
         scratch_shapes=[
+            pltpu.VMEM((owners, rows + EXTRA, sticks), jnp.bfloat16),
             pltpu.VMEM((owners, 2 * sticks, wide), jnp.bfloat16),
             grid_part,
             grid_part,
@@ -362,8 +385,8 @@
             pltpu.VMEM((PLANES, size, LANES), jnp.float32),
             pltpu.VMEM((PLANES, size, LANES), jnp.float32),
             pltpu.VMEM((owners, rows, sticks), jnp.bfloat16),
-            pltpu.SemaphoreType.DMA((groups + 1, owners - 1)),
-            pltpu.SemaphoreType.DMA((groups + 1, owners - 1)),
+            pltpu.SemaphoreType.DMA((groups + 2, owners - 1)),
+            pltpu.SemaphoreType.DMA((groups + 2, owners - 1)),
         ],
         compiler_params=pltpu.CompilerParams(
             collective_id=0, has_side_effects=True, vmem_limit_bytes=48 * 1024 * 1024
@@ -371,7 +394,7 @@
         cost_estimate=pl.CostEstimate(
             flops=40 * 10**9, bytes_accessed=8 * 10**6, transcendentals=0
         ),
-    )(received, potential, lines_table, halves, extra)
+    )(sent, potential, lines_table, halves, extra)
 
 
 def gathered_bands(array, mesh_bands):
@@ -416,8 +439,6 @@
     stick_count = stick_column.shape[0]
     owners = grid_size // slab_depth
     bands = orbitals.shape[0]
-    forward = dft_table(grid_size, 1.0, 1.0)
-    inverse = dft_table(grid_size, -1.0, 1.0 / grid_size)
     plane_index = sphere_slot // stick_count
     stick_index = sphere_slot % stick_count
     plane_hot = one_hot_rows(plane_index, grid_size)
@@ -439,10 +460,15 @@
     stick_buffer = jnp.einsum(
         "bpi,zi,si->pzbs", orbitals, plane_hot, stick_hot, preferred_element_type=jnp.float32
     ).astype(jnp.bfloat16)
-    along_z = apply_dft(stick_buffer[0], stick_buffer[1], forward, "zbs,zk->kbs")
-    pieces = [part.astype(jnp.bfloat16).reshape(owners, -1, stick_count) for part in along_z]
+    forward, backward = column_tables(grid_size)
+    along_z = jnp.dot(
+        forward,
+        stick_buffer.reshape(2 * grid_size, bands * stick_count),
+        preferred_element_type=jnp.float32,
+    ).astype(jnp.bfloat16)
+    along_z = along_z.reshape(2, owners, slab_depth * bands, stick_count)
+    pieces = [along_z[0], along_z[1]]
     sent = jnp.concatenate(pieces + [coords], axis=1)
-    received = lax.all_to_all(sent, "fft", split_axis=0, concat_axis=0, tiled=True)
     split = overlaps(subspace, previous, mesh_bands, owners)
     flat = split.reshape(owners, 1, -1)
     high = lax.reduce_precision(flat, 8, 7)
@@ -453,24 +479,23 @@
     both = jnp.pad(both, ((0, 0), (0, 0), (0, lanes - width)))
     both = both.reshape(owners, -1, stick_count)
     both = jnp.pad(both, ((0, 0), (0, EXTRA - both.shape[1]), (0, 0)))
-    returned = plane_work(received, potential, both, bands)
+    returned = plane_work(sent, potential, both, bands)
     rows = 2 * slab_depth * bands
     sums = returned[:, rows:].reshape(owners, -1)[:, :width].astype(jnp.float32)
     sums = jnp.sum(sums, axis=0)
     intersection = (sums[: width // 2] + sums[width // 2 :]).reshape(split.shape[1:])
-    stick_values = returned[:, :rows].reshape(owners, -1, 2, PLANES, bands, stick_count)
+    stick_values = returned[:, :rows].reshape(owners, -1, 2, PLANES, bands * stick_count)
+    stick_values = stick_values.transpose(2, 0, 1, 3, 4).reshape(2 * grid_size, -1)
+    columns = jnp.dot(backward, stick_values, preferred_element_type=jnp.float32)
+    columns = (columns * (1.0 / grid_size)).astype(jnp.bfloat16)
+    columns = columns.reshape(2, grid_size, bands, stick_count)
     picked = jnp.einsum(
-        "dgpzbs,si->pdgzbi", stick_values, stick_hot, preferred_element_type=jnp.float32
+        "pzbs,si->pzbi", columns, stick_hot, preferred_element_type=jnp.float32
     ).astype(jnp.bfloat16)
-    picked = picked.reshape(2, grid_size, bands, -1)
-    cosine_cols = jnp.einsum("zk,ki->zi", inverse[0], plane_hot, preferred_element_type=jnp.float32)
-    sine_cols = jnp.einsum("zk,ki->zi", inverse[1], plane_hot, preferred_element_type=jnp.float32)
-    pick_real = picked[0].astype(jnp.float32)
-    pick_imag = picked[1].astype(jnp.float32)
-    cosine_cols = cosine_cols[:, None]
-    sine_cols = sine_cols[:, None]
-    wave_real = jnp.sum(pick_real * cosine_cols - pick_imag * sine_cols, axis=0)
-    wave_imag = jnp.sum(pick_real * sine_cols + pick_imag * cosine_cols, axis=0)
+    levels = jnp.arange(grid_size, dtype=jnp.int32)[:, None]
+    here = (plane_index[None, :] == levels)[None, :, None, :]
+    waves = jnp.sum(jnp.where(here, picked.astype(jnp.float32), 0.0), axis=1)
+    wave_real, wave_imag = waves[0], waves[1]
     real_out = wave_real + kinetic * orbitals[:, 0].astype(jnp.float32)
     imag_out = wave_imag + kinetic * orbitals[:, 1].astype(jnp.float32)
     applied = jnp.stack([real_out, imag_out], axis=1).astype(jnp.bfloat16)

time: 109 us -> 88.9 us (0.82)
  local copies, waits for them, and re-layouts: 23.6 us -> 7.41 us
  Pallas kernels: 49.1 us -> 62.2 us
  matrix products: 17.8 us -> 10.5 us
  other arithmetic: 7.88 us -> 2.78 us
  starting transfers between devices: 9.36 us -> 4.48 us
    mul x4 -> x0, local copies, waits for them, and re-layouts: 20.5 us -> none  [fast_device(): wave_real = jnp.sum(pick_real * cosine_cols - pick_imag * sine_cols, axis=0)]
    pallas_call x1, Pallas kernels: 49.1 us -> 62.2 us  [plane_work(): pl.pallas_call(functools.partial(plane_kernel, slab), out_shape=jax.Shape...]
    dot_general x7 -> x3, matrix products: 13.7 us -> 4.91 us  [the longest x1 4.08 us: fast_device(): jnp.einsum('pzbs,si->pzbi', columns, stick_hot, preferred_element_type=jn...]
    all_to_all x1 -> x0, starting transfers between devices: 5.84 us -> none  [fast_device(): lax.all_to_all(sent, 'fft', split_axis=0, concat_axis=0, tiled=True)]
    reduce_sum x1 -> x0, other arithmetic: 4.76 us -> none  [fast_device(): wave_real = jnp.sum(pick_real * cosine_cols - pick_imag * sine_cols, axis=0)]
    slice x1, local copies, waits for them, and re-layouts: 0.09 us -> 1.66 us  [fast_device(): real_out = wave_real + kinetic * orbitals[:, 0].astype(jnp.float32)]
    dot_general x4, matrix products: 0.81 us -> 2.33 us  [overlaps(): jnp.einsum('jg,ig->ji', block.reshape(block.shape[0], -1), right, preferr...]
  transfers between devices with their start and end apart: 4 -> 3, of which waited for: 0 -> 0; matrix products, arithmetic and copies ran while one was open for 36% -> 15% of each run, Pallas kernels for 0% -> 0%
where the time goes in v2:
time: 88.9 us; the launch traced here: 88.4 us
  Pallas kernels  62.2 us (70%)
  matrix products  10.5 us (12%)
  local copies, waits for them, and re-layouts  7.41 us (8%)
  starting transfers between devices  4.48 us (5%)
  other arithmetic  2.78 us (3%)
  between operations  1.01 us (1%)
    pallas_call x1, Pallas kernels, plane_work(): pl.pallas_call(functools.partial(plane_kernel, slab), out_shape=jax.Shape...  62.2 us
    ppermute x3, starting transfers between devices, gathered_bands(): blocks.append(lax.ppermute(array, 'band', pairs))  4.48 us
    dot_general x1, matrix products, fast_device(): jnp.einsum('pzbs,si->pzbi', columns, stick_hot, preferred_element_type=jn...  4.08 us
    unnamed x27, local copies, waits for them, and re-layouts  3.07 us
    dot_general x1, matrix products, fast_device(): jnp.einsum('bpi,zi,si->pzbs', orbitals, plane_hot, stick_hot, preferred_e...  2.87 us
    dot_general x4, matrix products, overlaps(): jnp.einsum('jg,ig->ji', block.reshape(block.shape[0], -1), right, preferr...  2.33 us
  transfers between devices with their start and end apart: 3, of which 0 were waited for; matrix products, arithmetic and copies ran while one was open for 15% of the time, Pallas kernels for 0%

profile of v2, /device:TPU:0, one launch (start us, length us, event | category | flops | bytes accessed | tf_op | source)
XLA Modules:
  0.0 88.4 jit_solution(2847232542889917228)
XLA Ops:
  0.6 0.5 collective-permute-start.2
  1.2 2.6 %collective-permute-start.1 = (bf16[16,2,4096]{2,1,0:T(2,128)(2,1)}, bf16[16,2,4096]{2,1,0:T(2,128)(2,1)S(1)}, u32[]{:S(2)}, u32[]{:S(2)}) collective-permute-start(bf16[16,2,4096]{2,1,0:T(2,128)(2,1)} %param.14), channel_id=1, source_target_pairs={{16,0},{24,8},{0,16},{8,24},{17,1},{25,9},{1,17},{9,25},{18,2},{26... | collective-permute-start | bytes 786440 | tf_op jit(solution)/shard_map/ppermute | solution.py:405
  3.7 1.4 %collective-permute-start = (bf16[16,2,4096]{2,1,0:T(2,128)(2,1)}, bf16[16,2,4096]{2,1,0:T(2,128)(2,1)S(1)}, u32[]{:S(2)}, u32[]{:S(2)}) collective-permute-start(bf16[16,2,4096]{2,1,0:T(2,128)(2,1)} %param.14), channel_id=1, source_target_pairs={{8,0},{16,8},{24,16},{0,24},{9,1},{17,9},{25,17},{1,25},{10,2},{18... | collective-permute-start | bytes 786440 | tf_op jit(solution)/shard_map/ppermute | solution.py:405
  5.1 0.9 %convert_bitcast_fusion.1 = f32[4096,4,2]{0,2,1:T(2,128)S(1)} fusion(bf16[4,2,4096]{2,1,0:T(2,128)(2,1)} %param.10), kind=kLoop, calls=%fused_computation.30 | loop fusion | flops 32768 | bytes 196608 | tf_op jit(solution)/shard_map/convert.5
  6.0 1.7 %fusion.57 = (bf16[4,1,4096]{2,1,0:T(2,128)(2,1)S(1)}, bf16[4,1,4096]{2,1,0:T(2,128)(2,1)}) fusion(bf16[4,2,4096]{2,1,0:T(2,128)(2,1)} %param.10), kind=kLoop, calls=%fused_computation.90 | loop fusion | bytes 131072 | tf_op jit(solution)/shard_map/slice | solution.py:499
  7.7 1.0 %fusion.58 = (bf16[4,1,4096]{2,1,0:T(2,128)(2,1)S(1)}, bf16[4,1,4096]{2,1,0:T(2,128)(2,1)S(1)}) fusion(bf16[4,2,4096]{2,1,0:T(2,128)(2,1)} %param.15), kind=kLoop, calls=%fused_computation.91 | loop fusion | bytes 131072 | tf_op jit(solution)/shard_map/slice | solution.py:411
  8.7 0.1 fusion.55
  8.8 0.0 copy-start.6
  8.8 1.1 %copy.70 = bf16[2,8,2,4096]{3,1,2,0:T(8,128)(2,1)S(1)} copy(bf16[2,8,2,4096]{3,2,1,0:T(2,128)(2,1)} %bitcast.101) | data formatting | bytes 524288
  9.9 0.7 add_select_fusion
  10.7 0.2 convert_bitcast_fusion
  10.9 0.4 iota_compare_fusion
  11.3 0.0 copy-start.3
  11.3 2.9 %fusion.16 = bf16[2,192,4,128]{3,1,0,2:T(8,128)(2,1)S(1)} fusion(f32[4096,4,2]{0,2,1:T(2,128)S(1)} %convert_bitcast_fusion.1, f32[4096,128]{0,1:T(8,128)S(1)} %convert_bitcast_fusion, s32[4096]{0:T(1024)S(1)} %get-tuple-element.27), kind=kOutput, calls=%fused_computation.17 | convolution fusion | flops 1615790080 | bytes 2637824 | tf_op jit(solution)/shard_map/bpi,zi,si->pzbs/dot_general | solution.py:460
  14.2 0.0 copy-start.8
  14.2 0.0 copy-start.5
  14.2 0.3 copy.48
  14.5 0.0 copy-done.3
  14.6 0.4 fusion.15
  15.0 0.1 squeeze.22
  15.1 0.0 copy-start
  15.1 0.0 copy-start.1
  15.1 0.1 squeeze.23
  15.3 0.0 copy-done.8
  15.3 0.4 fusion.6
  15.8 0.0 copy-done.6
  15.8 0.2 convolution_bitcast_fusion.3
  16.0 0.0 copy-start.7
  16.0 0.0 copy-done.5
  16.1 0.0 collective-permute-done.2
  16.1 0.2 copy.73
  16.3 1.0 %convolution_bitcast_fusion = f32[16,8]{0,1:T(8,128)S(1)} fusion(bf16[16,8192]{1,0:T(8,128)(2,1)S(1)} %bitcast.107, bf16[4,4096]{1,0:T(4,128)(2,1)S(1)} %get-tuple-element.14, bf16[4,4096]{1,0:T(4,128)(2,1)S(1)} %bitcast.115, bf16[4,4096]{1,0:T(4,128)(2,1)} %copy-done.6), kind=kOutput, calls=%fused_computation.19 | convolution fusion | flops 2621440 | bytes 360960 | tf_op jit(solution)/shard_map/jg,ig->ji/dot_general | solution.py:422
  17.3 0.0 collective-permute-done.1
  17.3 0.2 copy.72
  17.4 1.0 %convolution_bitcast_fusion.1 = f32[16,8]{0,1:T(8,128)S(1)} fusion(bf16[16,8192]{1,0:T(8,128)(2,1)S(1)} %bitcast.108, bf16[4,4096]{1,0:T(4,128)(2,1)S(1)} %get-tuple-element.14, bf16[4,4096]{1,0:T(4,128)(2,1)S(1)} %bitcast.116, bf16[4,4096]{1,0:T(4,128)(2,1)} %copy-done.6), kind=kOutput, calls=%fused_computation.20 | convolution fusion | flops 2621440 | bytes 360960 | tf_op jit(solution)/shard_map/jg,ig->ji/dot_general | solution.py:422
  18.4 0.0 collective-permute-done
  18.4 0.2 copy.71
  18.5 0.0 copy-done.7
  18.6 0.2 convolution_bitcast_fusion.2
  18.8 0.1 concatenate.35
  18.8 0.1 constant_dynamic-slice_fusion
  18.9 0.1 reshape.146
  19.0 0.1 copy.50
  19.1 0.1 copy.51
  19.2 0.1 fusion.33.extra_ref
  19.3 0.0 copy-done
  19.3 0.0 copy-done.1
  19.3 0.0 copy-start.2
  19.3 62.2 %shard_map.113 = bf16[8,208,128]{2,1,0:T(8,128)(2,1)S(1)} custom-call(bf16[8,208,128]{2,1,0:T(8,128)(2,1)S(1)} %pad_maximum_fusion.sent_ref, f32[24,192,192]{2,1,0:T(8,128)} %pot_ref.1, bf16[2,192,512]{2,1,0:T(8,128)(2,1)S(1)} %copy-done, bf16[4,192,192]{2,1,0:T(8,128)(2,1)S(1)} %copy-done.1, bf16[8,16,128]{2,1,0:T(8,128)(2,1)S(1)} %fusion.33.extra_ref), custom_call_target="tpu_custom_call" | custom-call | flops 40000000000 | bytes 8000000 | tf_op jit(solution)/shard_map/pallas_call | solution.py:373
  81.5 0.2 reshape.152
  81.8 0.0 copy-done.2
  81.8 0.5 fusion.21
  82.2 0.3 reshape.159
  82.5 0.0 copy-start.4
  82.5 4.1 %select_reduce_fusion = f32[2,4,4096]{2,1,0:T(4,128)S(1)} fusion(pred[192,4096]{1,0:T(8,128)(4,1)S(1)} %iota_compare_fusion, s32[4096]{0:T(1024)S(1)} %get-tuple-element.26, bf16[2,192,4,128]{1,0,3,2:T(2,128)(2,1)S(1)} %reshape.159), kind=kOutput, calls=%fused_computation | convolution fusion | flops 1636270080 | bytes 1327104 | tf_op jit(solution)/shard_map/pzbs,si->pzbi/dot_general | solution.py:492
  86.6 0.0 copy-done.4
  86.6 0.1 fusion.30
  86.8 0.7 copy.59
  87.6 0.1 slice_add_fusion
  87.6 0.1 add.58
  87.7 0.7 copy.60
  (18 shorter events, 0.4 us)
Async XLA Ops:
  0.6 15.5 %collective-permute-start.2 = (bf16[16,2,4096]{2,1,0:T(2,128)(2,1)}, bf16[16,2,4096]{2,1,0:T(2,128)(2,1)S(1)}, u32[]{:S(2)}, u32[]{:S(2)}) collective-permute-start(bf16[16,2,4096]{2,1,0:T(2,128)(2,1)} %param.14), channel_id=1, source_target_pairs={{24,0},{0,8},{8,16},{16,24},{25,1},{1,9},{9,17},{17,25},{26,2},{2,... | collective-permute-start | bytes 786440 | tf_op jit(solution)/shard_map/ppermute | solution.py:405
  1.2 16.1 %collective-permute-start.1 = (bf16[16,2,4096]{2,1,0:T(2,128)(2,1)}, bf16[16,2,4096]{2,1,0:T(2,128)(2,1)S(1)}, u32[]{:S(2)}, u32[]{:S(2)}) collective-permute-start(bf16[16,2,4096]{2,1,0:T(2,128)(2,1)} %param.14), channel_id=1, source_target_pairs={{16,0},{24,8},{0,16},{8,24},{17,1},{25,9},{1,17},{9,25},{18,2},{26... | collective-permute-start | bytes 786440 | tf_op jit(solution)/shard_map/ppermute | solution.py:405
  3.7 14.7 %collective-permute-start = (bf16[16,2,4096]{2,1,0:T(2,128)(2,1)}, bf16[16,2,4096]{2,1,0:T(2,128)(2,1)S(1)}, u32[]{:S(2)}, u32[]{:S(2)}) collective-permute-start(bf16[16,2,4096]{2,1,0:T(2,128)(2,1)} %param.14), channel_id=1, source_target_pairs={{8,0},{16,8},{24,16},{0,24},{9,1},{17,9},{25,17},{1,25},{10,2},{18... | collective-permute-start | bytes 786440 | tf_op jit(solution)/shard_map/ppermute | solution.py:405
  8.8 7.0 %copy-start.6 = (bf16[4,4096]{1,0:T(4,128)(2,1)}, bf16[4,4096]{1,0:T(4,128)(2,1)S(1)}, u32[]{:S(2)}) copy-start(bf16[4,4096]{1,0:T(4,128)(2,1)S(1)} %get-tuple-element.15) | copy-start | bytes 98308
  11.3 3.2 %copy-start.3 = (bf16[384,384]{1,0:T(8,128)(2,1)S(1)}, bf16[384,384]{1,0:T(8,128)(2,1)}, u32[]{:S(2)}) copy-start(bf16[384,384]{1,0:T(8,128)(2,1)} %constant.93.clone) | copy-start | bytes 884740
  14.2 1.1 %copy-start.8 = (s32[128]{0:T(128)S(1)}, s32[128]{0:T(128)}, u32[]{:S(2)}) copy-start(s32[128]{0:T(128)} %param.12) | copy-start | bytes 1540
  14.2 1.8 %copy-start.5 = (s32[4096]{0:T(1024)S(1)}, s32[4096]{0:T(1024)}, u32[]{:S(2)}) copy-start(s32[4096]{0:T(1024)} %param.11) | copy-start | bytes 49156
  15.1 4.2 %copy-start = (bf16[2,192,512]{2,1,0:T(8,128)(2,1)S(1)}, bf16[2,192,512]{2,1,0:T(8,128)(2,1)}, u32[]{:S(2)}) copy-start(bf16[2,192,512]{2,1,0:T(8,128)(2,1)} %constant.95.clone.line_ref) | copy-start | bytes 1179652
  15.1 4.2 %copy-start.1 = (bf16[4,192,192]{2,1,0:T(8,128)(2,1)S(1)}, bf16[4,192,192]{2,1,0:T(8,128)(2,1)}, u32[]{:S(2)}) copy-start(bf16[4,192,192]{2,1,0:T(8,128)(2,1)} %constant.96.clone.half_ref) | copy-start | bytes 884740
  16.0 2.5 %copy-start.7 = (bf16[4,4096]{1,0:T(4,128)(2,1)S(1)}, bf16[4,4096]{1,0:T(4,128)(2,1)}, u32[]{:S(2)}) copy-start(bf16[4,4096]{1,0:T(4,128)(2,1)} %copy-done.6) | copy-start | bytes 98308
  19.3 62.5 %copy-start.2 = (bf16[384,384]{1,0:T(8,128)(2,1)S(1)}, bf16[384,384]{1,0:T(8,128)(2,1)}, u32[]{:S(2)}) copy-start(bf16[384,384]{1,0:T(8,128)(2,1)} %constant.103) | copy-start | bytes 884740
  82.5 4.1 %copy-start.4 = (bf16[4,1,4096]{2,1,0:T(2,128)(2,1)S(1)}, bf16[4,1,4096]{2,1,0:T(2,128)(2,1)}, u32[]{:S(2)}) copy-start(bf16[4,1,4096]{2,1,0:T(2,128)(2,1)} %get-tuple-element.21) | copy-start | bytes 98308
